TPU v7x, 32 devices: a 4x4x1 block of a 4x4x8 slice. The times are simulated.
32 devices in a mesh: dp: 1 (over z), tp: 32 (over y, x, core).
Axes of the slice: x: 4, y: 4, z: 1, core: 2. Of those that a mesh axis runs over, the one named last changes fastest.
The devices are a block of a 4x4x8 slice.
Arguments:
- hidden: bfloat16 [8192, 4096], P(('dp', 'tp'))
- ln_gain: float32 [4096], replicated
- ln_bias: float32 [4096], replicated
- out_embed: bfloat16 [32768, 4096], P('tp')
- vocab_valid: int32 [32768], P('tp')
- targets: int32 [8192], P(('dp', 'tp'))
- loss_mask: int32 [8192], P(('dp', 'tp'))
Outputs:
- output 1: float32 [8192], P(('dp', 'tp'))
- output 2: float32 [1], P('dp')
- output 3: bfloat16 [8192, 4096], P(('dp', 'tp'))
- output 4: float32 [32768, 4096], P(('dp', 'tp'))
- output 5: float32 [4096], P('dp')
- output 6: float32 [4096], P('dp')
All inputs are finite; a program needn't handle non-finite values.
Results may differ from a plain program's by a relative error of at most 0.001.
Values are sent between devices in bfloat16 or wider.
A program may use at most 768 MiB of HBM per device.

v0:
```python
import jax
import jax.numpy as jnp
from jax import lax
from jax.sharding import PartitionSpec as P

SOFT_CAP = 30.0
Z_COEF = 1e-4
LN_EPS = 1e-5


def layer_norm(h_float, ln_gain, ln_bias):
    mean_val = jnp.mean(h_float, axis=-1, keepdims=True)
    centered = h_float - mean_val
    var_val = jnp.mean(centered * centered, axis=-1, keepdims=True)
    return centered * lax.rsqrt(var_val + LN_EPS) * ln_gain + ln_bias


def solution(mesh):
    def group_step(hidden, ln_gain, ln_bias, out_embed, vocab_valid, targets, loss_mask):
        rows_loc = hidden.shape[0]
        vocab_loc = out_embed.shape[0]
        shard_idx = lax.axis_index("tp")
        normed, ln_back = jax.vjp(layer_norm, hidden.astype(jnp.float32), ln_gain, ln_bias)
        x_all = lax.all_gather(normed.astype(jnp.bfloat16), "tp", axis=0, tiled=True)
        tgt_all = lax.all_gather(targets, "tp", axis=0, tiled=True)
        mask_all = lax.all_gather(loss_mask, "tp", axis=0, tiled=True).astype(jnp.float32)
        logits = lax.dot_general(x_all, out_embed, (((1,), (1,)), ((), ())), preferred_element_type=jnp.float32)
        tanh_val = jnp.tanh(logits / SOFT_CAP)
        capped = SOFT_CAP * tanh_val
        col_ok = (vocab_valid != 0)[None, :]
        masked = jnp.where(col_ok, capped, -SOFT_CAP)
        glob_max = lax.pmax(jnp.max(masked, axis=1), "tp")
        exp_vals = jnp.where(col_ok, jnp.exp(masked - glob_max[:, None]), 0.0)
        col_ids = shard_idx * vocab_loc + jnp.arange(vocab_loc)
        is_target = tgt_all[:, None] == col_ids[None, :]
        local_stats = jnp.stack([jnp.sum(exp_vals, axis=1), jnp.sum(jnp.where(is_target, capped, 0.0), axis=1)])
        group_stats = lax.psum(local_stats, "tp")
        sum_exp = group_stats[0]
        lse = glob_max + jnp.log(sum_exp)
        tok_count = jnp.sum(mask_all)
        loss_all = (lse - group_stats[1] + Z_COEF * lse * lse) * mask_all
        mean_loss = jnp.sum(loss_all) / tok_count
        tok_coef = mask_all / tok_count
        prob_coef = (1.0 + 2.0 * Z_COEF * lse) * tok_coef / sum_exp
        d_capped = prob_coef[:, None] * exp_vals - jnp.where(is_target, tok_coef[:, None], 0.0)
        d_logits = (d_capped * (1.0 - tanh_val * tanh_val)).astype(jnp.bfloat16)
        d_embed = lax.dot_general(d_logits, x_all, (((0,), (0,)), ((), ())), preferred_element_type=jnp.float32)
        dx_part = jnp.dot(d_logits, out_embed, preferred_element_type=jnp.float32)
        d_normed = lax.psum_scatter(dx_part, "tp", scatter_dimension=0, tiled=True)
        d_hidden, gain_part, bias_part = ln_back(d_normed)
        d_gain = lax.psum(gain_part, "tp")
        d_bias = lax.psum(bias_part, "tp")
        tok_loss = lax.dynamic_slice_in_dim(loss_all, shard_idx * rows_loc, rows_loc)
        return tok_loss, mean_loss.reshape(1), d_hidden.astype(jnp.bfloat16), d_embed, d_gain, d_bias

    row_spec = P(("dp", "tp"))
    mat_spec = P(("dp", "tp"), None)
    return jax.shard_map(group_step, mesh=mesh, in_specs=(mat_spec, P(None), P(None), P("tp", None), P("tp"), row_spec, row_spec), out_specs=(row_spec, P("dp"), mat_spec, mat_spec, P("dp"), P("dp")), check_vma=False)
```

profile of v0, /device:TPU:97, one launch (start us, length us, event | category | flops | bytes accessed | tf_op | source)
XLA Modules:
  0.0 1160.5 jit_solution(5807697916136179104)
XLA Ops:
  7.2 0.1 all-gather.4.cloned.1.call-start
  7.2 2.0 convert_reduce_fusion
  9.2 0.0 copy-start.2
  9.2 2.3 fusion.15
  11.5 0.0 copy-start.4
  11.5 3.9 fusion.13
  15.5 0.1 all-gather.4.cloned.1.call-update
  15.5 0.1 all-reduce.4.cloned.1.call-start
  15.6 32.7 %all-gather.1 = s32[32,1,256]{2,1,0:T(1,128)S(1)} all-gather(s32[1,1,256]{2,1,0:T(1,128)} %bitcast.24), channel_id=1, replica_groups=mesh['dp'=1,'tp'=32] {'tp'}, dimensions={0}, use_global_device_ids=true | all-gather | bytes 33792 | tf_op jit(solution)/shard_map/all_gather | solution.py:26
  48.4 32.1 %all-gather = s32[32,1,256]{2,1,0:T(1,128)S(1)} all-gather(s32[1,1,256]{2,1,0:T(1,128)} %bitcast.25), channel_id=1, replica_groups=mesh['dp'=1,'tp'=32] {'tp'}, dimensions={0}, use_global_device_ids=true | all-gather | bytes 33792 | tf_op jit(solution)/shard_map/all_gather | solution.py:25
  80.4 0.7 broadcast_compare_fusion
  81.1 135.0 %all-gather.4.cloned.1.call-done = bf16[8192,4096]{1,0:T(8,128)(2,1)} async-done(((bf16[256,4096]{1,0:T(8,128)(2,1)}), bf16[8192,4096]{1,0:T(8,128)(2,1)}) %all-gather.4.cloned.1.call-update) | async-done | bytes 67108880 | tf_op jit(solution)/shard_map/all_gather | solution.py:24
  216.2 80.2 %select_reduce_fusion = (f32[8192]{0:T(1024)S(1)}, f32[8192,1024]{0,1:T(8,128)}) fusion(pred[1024]{0:T(1024)(128)(4,1)S(1)} %broadcast_compare_fusion, bf16[8192,4096]{1,0:T(8,128)(2,1)} %all-gather.4.cloned.1.call-done, bf16[1024,4096]{1,0:T(8,128)(2,1)} %param.10), kind=kOutput, calls=%fused_computation.8 | convolution fusion | flops 68753022976 | bytes 109085696 | tf_op jit(solution)/shard_map/dot_general | solution.py:27
  296.4 54.8 %pmax.7 = f32[8192]{0:T(1024)S(1)} all-reduce(f32[8192]{0:T(1024)S(1)} %get-tuple-element.23), channel_id=1, replica_groups=mesh['dp'=1,'tp'=32] {'tp'}, use_global_device_ids=true, to_apply=%region_3.4 | all-reduce | flops 8192 | bytes 65536 | tf_op jit(solution)/shard_map/pmax | solution.py:32
  351.2 18.4 %fusion.5 = (f32[8192]{0:T(1024)S(1)}, f32[8192]{0:T(1024)S(1)}) fusion(f32[8192,1024]{0,1:T(8,128)} %get-tuple-element.24, f32[8192]{0:T(1024)S(1)} %pmax.7, pred[1024]{0:T(1024)(128)(4,1)S(1)} %broadcast_compare_fusion, s32[1024]{0:T(1024)S(1)} %iota_add_fusion, s32[8192]{0:T(1024)S(1)} %bitcast.16), kind=kLoop, calls=%fused_computation.10 | loop fusion | flops 75481088 | bytes 33690624 | tf_op jit(solution)/shard_map/reduce_sum | solution.py:36
  369.7 0.7 pad_maximum_fusion
  370.4 0.1 all-reduce.4.cloned.1.call-update
  370.4 0.1 reduce-scatter.4.cloned.1.call-start
  370.5 0.7 convert_reduce_fusion.1
  371.2 89.0 %all-reduce.4.cloned.1.call-done = f32[2,8192]{1,0:T(2,128)} async-done(((f32[2,8192]{1,0:T(2,128)}), f32[2,8192]{1,0:T(2,128)}) %all-reduce.4.cloned.1.call-update) | async-done | bytes 65552 | tf_op jit(solution)/shard_map/psum | solution.py:37
  460.2 1.0 fusion.27
  461.1 1.9 multiply_divide_fusion
  463.0 94.5 %fusion.22 = f32[8192,4096]{1,0:T(8,128)} fusion(bf16[1024,4096]{1,0:T(8,128)(2,1)} %param.10, f32[8192,1024]{0,1:T(8,128)} %get-tuple-element.24, f32[8192]{0:T(1024)S(1)} %get-tuple-element.16, f32[8192]{0:T(1024)S(1)} %get-tuple-element.15, s32[8192]{0:T(1024)S(1)} %bitcast.17, f32[8192]{0:T(1024)S(1)} %pmax.7, s32[1024]{0:T(1024)S(1)} %iota_add_fusion, ...), kind=kOutput, calls=%fused_computation.42 | convolution fusion | flops 68828528640 | bytes 176296960 | tf_op jit(solution)/shard_map/dot_general | solution.py:48
  557.5 0.1 reduce-scatter.4.cloned.1.call-update
  558.9 1.3 dynamic_slice.3
  560.2 24.1 %fusion.38 = bf16[8192,1024]{0,1:T(8,128)(2,1)} fusion(f32[8192,1024]{0,1:T(8,128)} %get-tuple-element.24, f32[8192]{0:T(1024)S(1)} %get-tuple-element.16, f32[8192]{0:T(1024)S(1)} %get-tuple-element.15, s32[8192]{0:T(1024)S(1)} %bitcast.18, f32[8192]{0:T(1024)S(1)} %pmax.7, s32[1024]{0:T(1024)S(1)} %iota_add_fusion, ...), kind=kLoop, calls=%fused_computation.5.clone.clone.1 | loop fusion | flops 109051904 | bytes 50467840 | tf_op jit(solution)/shard_map/dot_general | solution.py:47
  584.3 80.1 %fusion.20 = f32[1024,4096]{1,0:T(8,128)} fusion(bf16[8192,4096]{1,0:T(8,128)(2,1)} %all-gather.4.cloned.1.call-done, bf16[8192,1024]{0,1:T(8,128)(2,1)} %fusion.38), kind=kOutput, calls=%fused_computation.41 | convolution fusion | flops 68719476736 | bytes 100663296 | tf_op jit(solution)/shard_map/dot_general | solution.py:47
  664.4 433.6 %reduce-scatter.4.cloned.1.call-done = f32[256,4096]{1,0:T(8,128)} async-done(((f32[8192,4096]{1,0:T(8,128)}), f32[256,4096]{1,0:T(8,128)}) %reduce-scatter.4.cloned.1.call-update) | async-done | bytes 4194320
  1098.0 4.0 fusion.14
  1102.1 3.4 fusion.24
  1105.5 1.8 add_convert_fusion
  1107.3 45.2 %all-reduce.1 = (f32[4096]{0:T(1024)}, f32[4096]{0:T(1024)}) all-reduce(f32[4096]{0:T(1024)S(1)} %get-tuple-element.8, f32[4096]{0:T(1024)S(1)} %get-tuple-element.10), channel_id=1, replica_groups=mesh['dp'=1,'tp'=32] {'tp'}, use_global_device_ids=true, to_apply=%region_13.14 | all-reduce | flops 8192 | bytes 65536 | tf_op jit(solution)/shard_map/psum | solution.py:51
  (20 shorter events, 0.1 us)
Async XLA Ops:
  7.2 209.0 %all-gather.4.cloned.1.call-start = ((), (), s32[]{:S(2)}) async-start(), calls=%async_computation.1 | async-start | bytes 69206016 | tf_op jit(solution)/shard_map/all_gather | solution.py:24
  9.2 39.1 %copy-start.2 = (f32[256]{0:T(256)}, f32[256]{0:T(256)S(1)}, u32[]{:S(2)}) copy-start(f32[256]{0:T(256)S(1)} %broadcast_multiply_fusion) | copy-start | bytes 3076
  11.5 36.8 %copy-start.6 = (f32[256]{0:T(256)}, f32[256]{0:T(256)S(1)}, u32[]{:S(2)}) copy-start(f32[256]{0:T(256)S(1)} %fusion.15) | copy-start | bytes 3076
  11.5 36.8 %copy-start.4 = (f32[256]{0:T(256)}, f32[256]{0:T(256)S(1)}, u32[]{:S(2)}) copy-start(f32[256]{0:T(256)S(1)} %fusion.19) | copy-start | bytes 3076
  15.5 444.6 %all-reduce.4.cloned.1.call-start = ((), (), s32[]{:S(2)}) async-start(), calls=%async_computation.2 | async-start | bytes 131072 | tf_op jit(solution)/shard_map/psum | solution.py:37
  370.4 727.5 %reduce-scatter.4.cloned.1.call-start = ((), (), s32[]{:S(2)}) async-start(), calls=%async_computation.3 | async-start | bytes 138412032
  584.3 513.7 %copy-start = (bf16[256,4096]{1,0:T(8,128)(2,1)S(1)}, bf16[256,4096]{1,0:T(8,128)(2,1)}, u32[]{:S(2)}) copy-start(bf16[256,4096]{1,0:T(8,128)(2,1)} %param.7) | copy-start | bytes 6291460
  584.3 513.7 %copy-start.1 = (f32[4096]{0:T(1024)S(1)}, f32[4096]{0:T(1024)}, u32[]{:S(2)}) copy-start(f32[4096]{0:T(1024)} %param.8) | copy-start | bytes 49156
  584.3 513.7 %copy-start.3 = (f32[256]{0:T(256)S(1)}, f32[256]{0:T(256)}, u32[]{:S(2)}) copy-start(f32[256]{0:T(256)} %copy-done.2) | copy-start | bytes 3076
  584.3 513.7 %copy-start.5 = (f32[256]{0:T(256)S(1)}, f32[256]{0:T(256)}, u32[]{:S(2)}) copy-start(f32[256]{0:T(256)} %copy-done.4) | copy-start | bytes 3076
  584.3 517.7 %copy-start.7 = (f32[256]{0:T(256)S(1)}, f32[256]{0:T(256)}, u32[]{:S(2)}) copy-start(f32[256]{0:T(256)} %copy-done.6) | copy-start | bytes 3076
Sparse Core Ops, SparseCore 0:
  15.7 200.4 all-gather.3
  370.6 89.5 all-reduce.3
  557.7 540.2 reduce-scatter.3
where the time goes:
time: 1160 us
  waiting for transfers between devices  658 us (57%)
  matrix products  255 us (22%)
  blocking collectives  165 us (14%)
  other arithmetic  63.9 us (6%)
  between operations  16.7 us (1%)
    unnamed x4, waiting for transfers between devices  434 us
    all_gather x1, waiting for transfers between devices, group_step(): lax.all_gather(normed.astype(jnp.bfloat16), 'tp', axis=0, tiled=True)  135 us
    dot_general x1, matrix products, group_step(): dx_part = jnp.dot(d_logits, out_embed, preferred_element_type=jnp.float32)  94.5 us
    psum x1, waiting for transfers between devices, group_step(): group_stats = lax.psum(local_stats, 'tp')  89 us
    dot_general x1, matrix products, group_step(): lax.dot_general(x_all, out_embed, (((1,), (1,)), ((), ())), preferred_ele...  80.2 us
    dot_general x1, matrix products, group_step(): lax.dot_general(d_logits, x_all, (((0,), (0,)), ((), ())), preferred_elem...  80.1 us
    pmax x1, blocking collectives, group_step(): glob_max = lax.pmax(jnp.max(masked, axis=1), 'tp')  54.8 us
    psum x1, blocking collectives, group_step(): d_gain = lax.psum(gain_part, 'tp')  45.2 us
  transfers between devices with their start and end apart: 3, of which 3 were waited for; matrix products, arithmetic and copies ran while one was open for 9% of the time, Pallas kernels for 0%

commit v1 on v0

v1 whole, which is shorter than its diff:
```python
import functools
import math

import jax
import jax.numpy as jnp
from jax import lax
from jax.experimental import pallas as pl
from jax.experimental.pallas import tpu as pltpu
from jax.sharding import PartitionSpec as P

SOFT_CAP = 30.0
Z_COEF = 1e-4
LN_EPS = 1e-5

RINGS = 4
MESH = pl.DeviceIdType.MESH
F32 = jnp.float32
BF16 = jnp.bfloat16
HBM = pl.BlockSpec(memory_space=pltpu.HBM)
DMA = pltpu.SemaphoreType.DMA
VMEM_LIMIT = 66_000_000


def layer_norm(h_float, ln_gain, ln_bias):
    mean_val = jnp.mean(h_float, axis=-1, keepdims=True)
    centered = h_float - mean_val
    var_val = jnp.mean(centered * centered, axis=-1, keepdims=True)
    return centered * lax.rsqrt(var_val + LN_EPS) * ln_gain + ln_bias


class Place:
    def __init__(self, n):
        self.chips = n // 2
        self.side = math.isqrt(self.chips)
        idx = lax.axis_index("tp")
        self.idx = idx
        self.core = lax.rem(idx, 2)
        self.chip = idx // 2
        x = lax.rem(self.chip, self.side)
        y = self.chip // self.side
        d = lax.rem(x + y, self.side)
        self.pos = [self.side * y + d, self.side * x + d]
        self.partner = idx + 1 - 2 * self.core

    def chip_at(self, q, p):
        p = lax.rem(p + 2 * self.chips, self.chips)
        major = p // self.side
        minor = lax.rem(lax.rem(p, self.side) - major + self.side, self.side)
        return major * self.side + minor if q < 2 else minor * self.side + major

    def step(self, q, s):
        return self.chip_at(q, self.pos[q // 2] - s if q % 2 == 0 else self.pos[q // 2] + s)

    def ring_next(self, q):
        return self.step(q, -1) * 2 + self.core

    def ring_prev(self, q):
        return self.step(q, 1) * 2 + self.core

    def peer(self, d):
        return lax.rem(self.chip + d, self.chips) * 2 + self.core


def to(device):
    return dict(device_id={"tp": device}, device_id_type=MESH)


def meet(at):
    bar = pltpu.get_barrier_semaphore()

    def hello(d, _):
        pl.semaphore_signal(bar, inc=1, **to(at.peer(d)))
        return 0

    lax.fori_loop(1, at.chips, hello, 0)
    pl.semaphore_signal(bar, inc=1, **to(at.partner))
    pl.semaphore_wait(bar, at.chips)


def ring_lane(width, sub):
    lane = lax.broadcasted_iota(jnp.int32, (1, width), 1)
    return lax.rem(lane // sub, RINGS)


def pick(at, table, s, lane_ring):
    row = lax.broadcasted_iota(jnp.int32, table.shape, 0)
    owner = at.step(0, s)
    for q in range(1, RINGS):
        owner = jnp.where(lane_ring == q, at.step(q, s), owner)
    return jnp.sum(jnp.where(row == owner, table, jnp.zeros_like(table)), axis=0, keepdims=True)


def gather_kernel(n, x_ref, e_ref, vv_ref, meta_ref, g_ref, t_ref, ep_ref, vvp_ref, metas_ref, stats_ref,
                  emb, valid, tile, stage, metas, st,
                  send, recv, msend, mrecv, psend, precv, esem, lsem, tsem, osem):
    at = Place(n)
    chips = at.chips
    rows = x_ref.shape[0]
    half = rows // 2
    sub = half // RINGS
    voc = e_ref.shape[0]
    rb = stage.shape[1]
    blocks = 2 * voc // rb

    def ring(src, s, q, h):
        part = pl.ds(h * half + q * sub, sub)
        return pltpu.make_async_remote_copy(
            src_ref=src.at[part], dst_ref=g_ref.at[s + 1, part],
            send_sem=send.at[s, q, h], recv_sem=recv.at[s, q, h], **to(at.ring_next(q)))

    def load(s, h):
        part = pl.ds(h * half, half)
        return pltpu.make_async_copy(g_ref.at[s, part], tile.at[lax.rem(s, 2), part], lsem.at[lax.rem(s, 2), h])

    def tell(d):
        return pltpu.make_async_remote_copy(
            src_ref=meta_ref, dst_ref=metas.at[at.chip], send_sem=msend.at[d], recv_sem=mrecv.at[d], **to(at.peer(d)))

    own = pltpu.make_async_copy(e_ref, emb.at[pl.ds(0, voc)], esem.at[0])
    own_valid = pltpu.make_async_copy(vv_ref, valid.at[pl.ds(0, voc)], esem.at[1])
    own_meta = pltpu.make_async_copy(meta_ref, metas.at[at.chip], esem.at[2])
    own_x = [pltpu.make_async_copy(x_ref.at[pl.ds(h * half, half)], tile.at[0, pl.ds(h * half, half)], lsem.at[0, h])
             for h in range(2)]
    give = pltpu.make_async_remote_copy(
        src_ref=e_ref, dst_ref=emb.at[pl.ds(voc, voc)], send_sem=psend.at[0], recv_sem=precv.at[0], **to(at.partner))
    give_valid = pltpu.make_async_remote_copy(
        src_ref=vv_ref, dst_ref=valid.at[pl.ds(voc, voc)], send_sem=psend.at[1], recv_sem=precv.at[1], **to(at.partner))

    own.start()
    own_valid.start()
    own_meta.start()
    for c in own_x:
        c.start()
    meet(at)
    for h in range(2):
        for q in range(RINGS):
            ring(x_ref, 0, q, h).start()

    def tell_all(d, _):
        tell(d).start()
        return 0

    lax.fori_loop(1, chips, tell_all, 0)
    give.start()
    give_valid.start()
    st[...] = jnp.zeros_like(st)

    def hear(d, _):
        tell(d).wait_recv()
        return 0

    own_meta.wait()
    lax.fori_loop(1, chips, hear, 0)
    own.wait()
    own_valid.wait()

    lane_ring = ring_lane(rows, sub)
    row_id = lax.broadcasted_iota(jnp.int32, (rb, 1), 0)
    base = [at.idx * voc, at.partner * voc]
    table_row = lax.broadcasted_iota(jnp.int32, (chips, rows), 0)

    def put(s, b):
        return pltpu.make_async_copy(stage.at[b % 4], t_ref.at[s, pl.ds(b * rb, rb)], tsem.at[b % 4])

    def step(s, _):
        slot = lax.rem(s, 2)
        tgt = pick(at, metas[:, 0, :], s, lane_ring)
        for h in range(2):
            pltpu.make_async_copy(x_ref.at[pl.ds(0, half)], tile.at[slot, pl.ds(h * half, half)], lsem.at[slot, h]).wait()

        keep = pltpu.make_async_copy(tile.at[0], g_ref.at[0], osem.at[2])

        @pl.when(s == 0)
        def _():
            keep.start()

        def arrive(h):
            @pl.when(s < chips - 1)
            def _():
                for q in range(RINGS):
                    ring(x_ref, s, q, h).wait_recv()

                    @pl.when(s < chips - 2)
                    def _():
                        ring(g_ref.at[s + 1], s + 1, q, h).start()
                load(s + 1, h).start()

        sums = jnp.zeros((1, rows), F32)
        hits = jnp.zeros((1, rows), F32)
        for b in range(blocks):
            if b == 0:
                arrive(0)
            if b == blocks - 1:
                arrive(1)
            if b == blocks // 2:
                @pl.when(s == 0)
                def _():
                    give.wait_recv()
                    give_valid.wait_recv()
                    pltpu.make_async_copy(emb.at[pl.ds(voc, voc)], ep_ref, osem.at[0]).start()
                    pltpu.make_async_copy(valid.at[pl.ds(voc, voc)], vvp_ref, osem.at[1]).start()
            z = lax.dot_general(emb[pl.ds(b * rb, rb), :], tile[slot], (((1,), (1,)), ((), ())),
                                preferred_element_type=F32)
            t = jnp.tanh(z * (1.0 / SOFT_CAP))
            @pl.when(s > 0)
            def _():
                put(s, b).wait()
            stage[b % 4] = t
            put(s, b).start()
            capped = SOFT_CAP * t
            ok = valid[pl.ds(b * rb, rb), :]
            ex = jnp.exp(capped) * jnp.concatenate([ok] * (rows // ok.shape[1]), axis=1)
            sums += jnp.sum(ex, axis=0, keepdims=True)
            first = base[(b * rb) // voc] + (b * rb) % voc
            hits += jnp.sum(jnp.where(row_id + first == tgt, capped, 0.0), axis=0, keepdims=True)
        owner = at.step(0, s)
        for q in range(1, RINGS):
            owner = jnp.where(lane_ring == q, at.step(q, s), owner)
        mine = table_row == owner

        @pl.when(s == 0)
        def _():
            keep.wait()
        st[0] = jnp.where(mine, sums, st[0])
        st[1] = jnp.where(mine, hits, st[1])
        return 0

    lax.fori_loop(0, chips, step, 0)
    outs = [pltpu.make_async_copy(metas, metas_ref, osem.at[2]), pltpu.make_async_copy(st, stats_ref, osem.at[3])]
    for c in outs:
        c.start()

    def drain(s, _):
        for h in range(2):
            for q in range(RINGS):
                ring(x_ref, s, q, h).wait_send()
        return 0

    lax.fori_loop(0, chips - 1, drain, 0)

    def told(d, _):
        tell(d).wait_send()
        return 0

    lax.fori_loop(1, chips, told, 0)
    give.wait_send()
    give_valid.wait_send()
    for b in range(blocks):
        put(0, b).wait()
    pltpu.make_async_copy(emb.at[pl.ds(voc, voc)], ep_ref, osem.at[0]).wait()
    pltpu.make_async_copy(valid.at[pl.ds(voc, voc)], vvp_ref, osem.at[1]).wait()
    for c in outs:
        c.wait()


def gather(n, x, e, vv, meta):
    chips = n // 2
    rows, dim = x.shape
    voc = e.shape[0]
    rb = voc // 2
    blocks = 2 * voc // rb
    shapes = (
        jax.ShapeDtypeStruct((chips, rows, dim), BF16),
        jax.ShapeDtypeStruct((chips, 2 * voc, rows), F32),
        jax.ShapeDtypeStruct((voc, dim), BF16),
        jax.ShapeDtypeStruct(vv.shape, F32),
        jax.ShapeDtypeStruct((chips,) + meta.shape, jnp.int32),
        jax.ShapeDtypeStruct((2, chips, rows), F32),
    )
    flops = 2 * chips * rows * 2 * voc * dim
    return pl.pallas_call(
        functools.partial(gather_kernel, n),
        out_shape=shapes,
        in_specs=[HBM] * 4,
        out_specs=(HBM,) * len(shapes),
        scratch_shapes=[
            pltpu.VMEM((2 * voc, dim), BF16),
            pltpu.VMEM((2 * voc, vv.shape[1]), F32),
            pltpu.VMEM((2, rows, dim), BF16),
            pltpu.VMEM((4, rb, rows), F32),
            pltpu.VMEM((chips,) + meta.shape, jnp.int32),
            pltpu.VMEM((2, chips, rows), F32),
            DMA((chips, RINGS, 2)), DMA((chips, RINGS, 2)),
            DMA((chips,)), DMA((chips,)),
            DMA((2,)), DMA((2,)),
            DMA((3,)), DMA((2, 2)), DMA((4,)), DMA((4,)),
        ],
        compiler_params=pltpu.CompilerParams(collective_id=0, has_side_effects=True, vmem_limit_bytes=VMEM_LIMIT),
        cost_estimate=pl.CostEstimate(flops=flops, bytes_accessed=0, transcendentals=0),
        name="gather_logits",
    )(x, e, vv, meta)


def scatter_kernel(n, g_ref, t_ref, e_ref, ep_ref, vv_ref, vvp_ref, metas_ref, stats_ref,
                   dx_ref, de_ref, loss_ref,
                   emb, dzt, acc, land, stage, xcol, de_own, de_send, de_land, dzn, valid, stat_all, metas, coef, cnt, lossv,
                   send, recv, credit, ssend, srecv, csem, lsem, zsem, xsem, psend, precv, pcredit, osem, nsend, nrecv):
    at = Place(n)
    chips = at.chips
    rows, dim = dx_ref.shape
    half = rows // 2
    sub = half // RINGS
    voc = e_ref.shape[0]
    rb = stage.shape[1]
    blocks = 2 * voc // rb
    cols = xcol.shape[1]
    col_blocks = dim // cols
    units = 2 * chips

    def ring(k, q, h):
        src = pl.ds(pl.multiple_of(q * sub, sub), sub)
        return pltpu.make_async_remote_copy(
            src_ref=acc.at[h, lax.rem(k, 2), src], dst_ref=land.at[h, lax.rem(k, 2), src],
            send_sem=send.at[k, q, h], recv_sem=recv.at[k, q, h], **to(at.ring_next(q)))

    def share(d):
        return pltpu.make_async_remote_copy(
            src_ref=stats_ref, dst_ref=stat_all.at[at.chip], send_sem=ssend.at[d], recv_sem=srecv.at[d], **to(at.peer(d)))

    loads = [
        pltpu.make_async_copy(metas_ref, metas, lsem.at[0]),
        pltpu.make_async_copy(stats_ref, stat_all.at[at.chip], lsem.at[1]),
        pltpu.make_async_copy(vv_ref, valid.at[pl.ds(0, voc)], lsem.at[2]),
        pltpu.make_async_copy(vvp_ref, valid.at[pl.ds(voc, voc)], lsem.at[3]),
        pltpu.make_async_copy(e_ref, emb.at[pl.ds(0, voc)], lsem.at[4]),
        pltpu.make_async_copy(ep_ref, emb.at[pl.ds(voc, voc)], lsem.at[5]),
    ]
    for c in loads:
        c.start()

    def zload(o, b):
        return pltpu.make_async_copy(t_ref.at[lax.rem(o + 1, chips), pl.ds(b * rb, rb)], stage.at[b % 2], zsem.at[b % 2])

    zload(0, 0).start()
    meet(at)

    def share_all(d, _):
        share(d).start()
        return 0

    lax.fori_loop(1, chips, share_all, 0)

    loads[0].wait()
    mask = metas[:, 1, :].astype(F32)
    cnt[0] = jnp.full(cnt.shape[1:], jnp.sum(mask), F32)
    swap = pltpu.make_async_remote_copy(src_ref=cnt.at[0], dst_ref=cnt.at[1], send_sem=nsend, recv_sem=nrecv, **to(at.partner))
    swap.start()

    def hear(d, _):
        share(d).wait_recv()
        return 0

    loads[1].wait()
    lax.fori_loop(1, chips, hear, 0)
    swap.wait()
    total = cnt[0, 0:1, 0:1] + cnt[1, 0:1, 0:1]
    sum_exp = jnp.sum(stat_all[:, 0], axis=0)
    hits = jnp.sum(stat_all[:, 1], axis=0)
    lse = jnp.log(sum_exp)
    tok_coef = mask / total
    coef[0] = (1.0 + 2.0 * Z_COEF * lse) * tok_coef / sum_exp
    coef[1] = tok_coef
    loss = (lse - hits + Z_COEF * lse * lse) * mask
    table_row = lax.broadcasted_iota(jnp.int32, loss.shape, 0)
    own_loss = jnp.sum(jnp.where(table_row == at.chip, loss, 0.0), axis=0, keepdims=True)
    out_row = lax.broadcasted_iota(jnp.int32, lossv.shape, 0)
    lossv[...] = jnp.where(out_row == 0, own_loss, jnp.sum(own_loss) / total)
    out_loss = pltpu.make_async_copy(lossv, loss_ref, osem.at[2])
    out_loss.start()

    lane_ring = ring_lane(rows, sub)
    row_id = lax.broadcasted_iota(jnp.int32, (rb, 1), 0)
    base = [at.idx * voc, at.partner * voc]

    def d_logits(o):
        s = lax.rem(o + 1, chips)
        tgt = pick(at, metas[:, 0, :], s, lane_ring)
        ca = pick(at, coef[0], s, lane_ring)
        cb = pick(at, coef[1], s, lane_ring)
        lanes = pl.ds(pl.multiple_of(s * rows, rows), rows)
        for b in range(blocks):
            zload(o, b).wait()
            if b + 1 < blocks:
                zload(o, b + 1).start()
            else:
                @pl.when(o + 1 < chips)
                def _():
                    zload(o + 1, 0).start()
            t = stage[b % 2]
            ok = valid[pl.ds(b * rb, rb), :]
            ex = jnp.exp(SOFT_CAP * t) * jnp.concatenate([ok] * (rows // ok.shape[1]), axis=1)
            first = base[(b * rb) // voc] + (b * rb) % voc
            d_cap = ca * ex - jnp.where(row_id + first == tgt, cb, 0.0)
            dzt[pl.ds(b * rb, rb), lanes] = (d_cap * (1.0 - t * t)).astype(BF16)

    nb = 512

    def d_x(k, h):
        s = lax.rem(k, chips)
        lanes = pl.ds(pl.multiple_of(s * rows + h * half, half), half)
        for r in range(2 * voc // half):
            dzn[:, pl.ds(r * half, half)] = dzt[pl.ds(r * half, half), lanes].T

        def block(j, _):
            c = pl.ds(pl.multiple_of(j * nb, nb), nb)
            acc[h, lax.rem(k, 2), :, c] = jnp.dot(dzn[...], emb[:, c], preferred_element_type=F32)
            return 0

        lax.fori_loop(0, dim // nb, block, 0)

    def xload(b):
        return pltpu.make_async_copy(g_ref.at[:, pl.ds(pl.multiple_of(b * cols, cols), cols)], xcol, xsem)

    def give(b):
        return pltpu.make_async_remote_copy(src_ref=de_send, dst_ref=de_land, send_sem=psend, recv_sem=precv, **to(at.partner))

    def out_de(b):
        return pltpu.make_async_copy(de_own.at[lax.rem(b, 2)],
                                     de_ref.at[:, pl.ds(pl.multiple_of(b * cols, cols), cols)], osem.at[lax.rem(b, 2)])

    rc = 512

    def de_finish(b):
        give(b).wait_recv()
        slot = lax.rem(b, 2)
        de_own[slot] = de_own[slot] + de_land[...]

        @pl.when(b < col_blocks - 1)
        def _():
            pl.semaphore_signal(pcredit, inc=1, **to(at.partner))
        out_de(b).start()

    def de_block(b):
        xload(b).wait()
        slot = lax.rem(b, 2)

        @pl.when(b > 0)
        def _():
            give(b).wait_send()

        def part(i, _):
            r = pl.ds(pl.multiple_of(i * rc, rc), rc)
            de_send[r] = jnp.dot(dzt[pl.ds(pl.multiple_of(voc + i * rc, rc), rc), :], xcol[...], preferred_element_type=F32)
            return 0

        lax.fori_loop(0, voc // rc, part, 0)

        @pl.when(b > 0)
        def _():
            pl.semaphore_wait(pcredit, 1)
        give(b).start()

        @pl.when(b >= 2)
        def _():
            out_de(b).wait()

        def part2(i, _):
            r = pl.ds(pl.multiple_of(i * rc, rc), rc)
            de_own[slot, r] = jnp.dot(dzt[r, :], xcol[...], preferred_element_type=F32)
            return 0

        lax.fori_loop(0, voc // rc, part2, 0)

        @pl.when(b < col_blocks - 1)
        def _():
            xload(b + 1).start()

    for c in loads[2:4]:
        c.wait()
    d_logits(0)
    for c in loads[4:]:
        c.wait()
    d_x(1, 0)
    d_x(1, 1)
    first_de = units - 1 - col_blocks

    def unit(u, _):
        k = 1 + u // 2
        h = lax.rem(u, 2)

        @pl.when(k > 1)
        def _():
            for q in range(RINGS):
                ring(k - 1, q, h).wait_recv()

            def add(i, _):
                r = pl.ds(pl.multiple_of(i * 8, 8), 8)
                acc[h, lax.rem(k, 2), r] += land[h, lax.rem(k - 1, 2), r]
                return 0

            lax.fori_loop(0, half // 8, add, 0)

            @pl.when(k < chips - 1)
            def _():
                for q in range(RINGS):
                    pl.semaphore_signal(credit.at[q, h], inc=1, **to(at.ring_prev(q)))

        @pl.when(k < chips)
        def _():
            for q in range(RINGS):
                @pl.when(k > 2)
                def _():
                    pl.semaphore_wait(credit.at[q, h], 1)
                ring(k, q, h).start()

        @pl.when(u < chips - 1)
        def _():
            d_logits(u + 1)

        @pl.when(u == first_de - 1)
        def _():
            xload(0).start()

        @pl.when(k < chips)
        def _():
            @pl.when(k > 1)
            def _():
                for q in range(RINGS):
                    ring(k - 1, q, h).wait_send()
            d_x(k + 1, h)

        @pl.when((u > first_de) & (u <= first_de + col_blocks))
        def _():
            de_finish(u - first_de - 1)

        @pl.when((u >= first_de) & (u < first_de + col_blocks))
        def _():
            de_block(u - first_de)
        return 0

    lax.fori_loop(0, units, unit, 0)
    outs = [pltpu.make_async_copy(acc.at[h, 0], dx_ref.at[pl.ds(h * half, half)], csem.at[h]) for h in range(2)]
    for c in outs:
        c.start()
    for h in range(2):
        for q in range(RINGS):
            ring(chips - 1, q, h).wait_send()

    def shared(d, _):
        share(d).wait_send()
        return 0

    lax.fori_loop(1, chips, shared, 0)
    give(0).wait_send()
    out_de(0).wait()
    out_de(1).wait()
    out_loss.wait()
    for c in outs:
        c.wait()


def scatter(n, g, t, e, ep, vv, vvp, metas, stats):
    chips, rows, dim = g.shape
    g = g.reshape(-1, dim)
    voc = e.shape[0]
    half = rows // 2
    rb, cols = 512, 256
    shapes = (
        jax.ShapeDtypeStruct((rows, dim), F32),
        jax.ShapeDtypeStruct((voc, dim), F32),
        jax.ShapeDtypeStruct((8, rows), F32),
    )
    flops = 4 * chips * rows * 2 * voc * dim
    return pl.pallas_call(
        functools.partial(scatter_kernel, n),
        out_shape=shapes,
        in_specs=[HBM] * 8,
        out_specs=(HBM,) * len(shapes),
        scratch_shapes=[
            pltpu.VMEM((2 * voc, dim), BF16),
            pltpu.VMEM((2 * voc, chips * rows), BF16),
            pltpu.VMEM((2, 2, half, dim), F32),
            pltpu.VMEM((2, 2, half, dim), F32),
            pltpu.VMEM((2, rb, rows), F32),
            pltpu.VMEM((chips * rows, cols), BF16),
            pltpu.VMEM((2, voc, cols), F32),
            pltpu.VMEM((voc, cols), F32),
            pltpu.VMEM((voc, cols), F32),
            pltpu.VMEM((half, 2 * voc), BF16),
            pltpu.VMEM((2 * voc, vv.shape[1]), F32),
            pltpu.VMEM((chips, 2, chips, rows), F32),
            pltpu.VMEM(metas.shape, jnp.int32),
            pltpu.VMEM((2, chips, rows), F32),
            pltpu.VMEM((2, 8, 128), F32),
            pltpu.VMEM((8, rows), F32),
            DMA((chips, RINGS, 2)), DMA((chips, RINGS, 2)), pltpu.SemaphoreType.REGULAR((RINGS, 2)),
            DMA((chips,)), DMA((chips,)), DMA((2,)), DMA((6,)), DMA((2,)), DMA,
            DMA, DMA, pltpu.SemaphoreType.REGULAR, DMA((3,)), DMA, DMA,
        ],
        compiler_params=pltpu.CompilerParams(collective_id=1, has_side_effects=True, vmem_limit_bytes=VMEM_LIMIT),
        cost_estimate=pl.CostEstimate(flops=flops, bytes_accessed=0, transcendentals=0),
        name="scatter_grads",
    )(g, t, e, ep, vv, vvp, metas, stats)


def total_kernel(n, p_ref, o_ref, part, pair, land, whole, psend, precv, send, recv, hsend, hrecv):
    at = Place(n)
    rows = p_ref.shape[0]
    half = rows // 2
    meet(at)
    swap = pltpu.make_async_remote_copy(src_ref=p_ref, dst_ref=pair, send_sem=psend, recv_sem=precv, **to(at.partner))
    swap.start()
    swap.wait()
    mine = pl.ds(pl.multiple_of(at.core * half, 8), half)
    part[...] = p_ref[mine] + pair[mine]
    land[at.chip] = part[...]

    def send_to(d):
        return pltpu.make_async_remote_copy(
            src_ref=part, dst_ref=land.at[at.chip], send_sem=send.at[d], recv_sem=recv.at[d], **to(at.peer(d)))

    def start(d, _):
        send_to(d).start()
        return 0

    def wait(d, _):
        send_to(d).wait()
        return 0

    lax.fori_loop(1, at.chips, start, 0)
    lax.fori_loop(1, at.chips, wait, 0)
    whole[mine] = jnp.sum(land[...], axis=0)
    back = pltpu.make_async_remote_copy(src_ref=whole.at[mine], dst_ref=whole.at[mine], send_sem=hsend, recv_sem=hrecv, **to(at.partner))
    back.start()
    back.wait()
    o_ref[...] = whole[...]


def total(n, p):
    chips = n // 2
    half = p.shape[0] // 2
    vm = pl.BlockSpec(memory_space=pltpu.VMEM)
    return pl.pallas_call(
        functools.partial(total_kernel, n),
        out_shape=jax.ShapeDtypeStruct(p.shape, F32),
        in_specs=[vm],
        out_specs=vm,
        scratch_shapes=[
            pltpu.VMEM((half, p.shape[1]), F32),
            pltpu.VMEM(p.shape, F32),
            pltpu.VMEM((chips, half, p.shape[1]), F32),
            pltpu.VMEM(p.shape, F32),
            DMA, DMA, DMA((chips,)), DMA((chips,)), DMA, DMA,
        ],
        compiler_params=pltpu.CompilerParams(collective_id=2, has_side_effects=True),
        name="small_totals",
    )(p)


def solution(mesh):
    n = mesh.shape["tp"]

    def group_step(hidden, ln_gain, ln_bias, out_embed, vocab_valid, targets, loss_mask):
        rows, dim = hidden.shape
        normed, ln_back = jax.vjp(layer_norm, hidden.astype(F32), ln_gain, ln_bias)
        x = normed.astype(BF16)
        vv = jnp.broadcast_to((vocab_valid != 0).astype(F32)[:, None], (vocab_valid.shape[0], 128))
        meta = jnp.concatenate([targets[None], loss_mask[None], jnp.zeros((6, rows), jnp.int32)], axis=0)
        g, t, ep, vvp, metas, stats = gather(n, x, out_embed, vv, meta)
        dx, d_embed, loss = scatter(n, g, t, out_embed, ep, vv, vvp, metas, stats)
        d_hidden, gain_part, bias_part = ln_back(dx)
        lanes = 128
        parts = jnp.concatenate([gain_part.reshape(-1, lanes), bias_part.reshape(-1, lanes),
                                 jnp.broadcast_to(loss[1:2, :lanes], (16, lanes))], axis=0)
        sums = total(n, parts)
        k = dim // lanes
        return (loss[0], sums[2 * k, :1], d_hidden.astype(BF16), d_embed,
                sums[:k].reshape(-1), sums[k:2 * k].reshape(-1))

    row_spec = P(("dp", "tp"))
    mat_spec = P(("dp", "tp"), None)
    return jax.shard_map(
        group_step, mesh=mesh,
        in_specs=(mat_spec, P(None), P(None), P("tp", None), P("tp"), row_spec, row_spec),
        out_specs=(row_spec, P("dp"), mat_spec, mat_spec, P("dp"), P("dp")), check_vma=False)
```

time: 1160 us -> 621 us (0.54)
  waiting for transfers between devices: 658 us -> 0 us
  Pallas kernels: 0 us -> 583 us
  matrix products: 255 us -> 0 us
  blocking collectives: 165 us -> 0 us
  other arithmetic: 63.9 us -> 15.9 us
  local copies, waits for them, and re-layouts: 2.33 us -> 18.5 us
  between operations: 16.7 us -> 0.86 us
    pallas_call x0 -> x3, Pallas kernels: none -> 583 us  [the longest x1 365 us: scatter(): pl.pallas_call(functools.partial(scatter_kernel, n), out_shape=shapes, in...]
    unnamed x4 -> x0, waiting for transfers between devices: 434 us -> none
    dot_general x3 -> x0, matrix products: 255 us -> none  [the longest x1 94.5 us: group_step(): dx_part = jnp.dot(d_logits, out_embed, preferred_element_type=jnp.float32)]
    all_gather x1 -> x0, waiting for transfers between devices: 135 us -> none  [group_step(): lax.all_gather(normed.astype(jnp.bfloat16), 'tp', axis=0, tiled=True)]
    psum x1 -> x0, waiting for transfers between devices: 89 us -> none  [group_step(): group_stats = lax.psum(local_stats, 'tp')]
    all_gather x2 -> x0, blocking collectives: 64.8 us -> none  [the longest x1 32.7 us: group_step(): lax.all_gather(loss_mask, 'tp', axis=0, tiled=True).astype(jnp.float32)]
    pmax x1 -> x0, blocking collectives: 54.8 us -> none  [group_step(): glob_max = lax.pmax(jnp.max(masked, axis=1), 'tp')]
    psum x1 -> x0, blocking collectives: 45.2 us -> none  [group_step(): d_gain = lax.psum(gain_part, 'tp')]
  transfers between devices with their start and end apart: 3 -> 0, of which waited for: 3 -> 0; matrix products, arithmetic and copies ran while one was open for 9% -> 0% of each run, Pallas kernels for 0% -> 0%
where the time goes in v1:
time: 621 us; the launch traced here: 619 us
  Pallas kernels  583 us (94%)
  local copies, waits for them, and re-layouts  18.5 us (3%)
  other arithmetic  15.9 us (3%)
    pallas_call x1, Pallas kernels, scatter(): pl.pallas_call(functools.partial(scatter_kernel, n), out_shape=shapes, in...  365 us
    pallas_call x1, Pallas kernels, gather(): pl.pallas_call(functools.partial(gather_kernel, n), out_shape=shapes, in_...  201 us
    pallas_call x1, Pallas kernels, total(): pl.pallas_call(functools.partial(total_kernel, n), out_shape=jax.ShapeDty...  16.9 us

profile of v1, /device:TPU:97, one launch (start us, length us, event | category | flops | bytes accessed | tf_op | source)
XLA Modules:
  0.0 618.7 jit_solution(17804156968338684663)
XLA Ops:
  0.6 0.0 copy-start
  0.6 0.0 copy-start.3
  0.7 0.0 copy-start.13
  0.7 0.0 copy-start.14
  0.7 0.0 copy-start.12
  0.7 0.0 copy-start.7
  0.7 0.1 pad.5.clone
  0.8 2.1 convert_reduce_fusion
  2.9 0.0 copy-start.5
  2.9 2.3 fusion.9
  5.2 0.6 copy-done.10
  5.8 0.7 add_add_fusion.1.meta_ref
  6.4 1.0 broadcast_in_dim.32.vv_ref
  7.5 0.0 copy-done.3
  7.5 0.0 copy-done.7
  7.5 2.4 fusion.7.x_ref
  9.8 201.4 %gather_logits.1 = (bf16[16,256,4096]{2,1,0:T(8,128)(2,1)}, f32[16,2048,256]{2,1,0:T(8,128)}, bf16[1024,4096]{1,0:T(8,128)(2,1)}, f32[1024,128]{1,0:T(8,128)}, s...) custom-call(bf16[256,4096]{1,0:T(8,128)(2,1)} %fusion.7.x_ref, bf16[1024,4096]{1,0:T(8,128)(2,1)} %e_ref.3, ...), custom_call_target="tpu_custom_call" | custom-call | flops 68719476736 | tf_op jit(solution)/shard_map/gather_logits/pallas_call | solution.py:271
  211.2 0.0 copy-start.4
  211.2 0.0 copy-start.6
  211.2 365.2 %scatter_grads.1 = (f32[256,4096]{1,0:T(8,128)}, f32[1024,4096]{1,0:T(8,128)}, f32[8,256]{1,0:T(8,128)}) custom-call(bf16[4096,4096]{1,0:T(8,128)(2,1)} %bitcast.18, f32[16,2048,256]{2,1,0:T(8,128)} %get-tuple-element.16.t_ref, bf16[1024,4096]{1,0:T(8,128)(2,1)} %e_ref.3, bf16[1024,4096]{1,0:T(8,128)(2,1)} %get-tuple-element.17.ep_ref, ...), custom_call_target="tpu_custom_call" | custom-call | flops 137438953472 | tf_op jit(solution)/shard_map/scatter_grads/pallas_call | solution.py:564
  576.5 0.0 copy-start.1
  576.5 0.8 slice_bitcast_fusion.2
  577.3 1.7 slice.15
  579.0 0.0 copy-done.4
  579.0 4.7 fusion.10
  583.8 1.3 fusion.12
  585.1 1.8 add_convert_fusion
  586.9 0.6 pad_maximum_fusion.p_ref
  587.5 16.9 %small_totals.1 = f32[80,128]{1,0:T(8,128)} custom-call(f32[80,128]{1,0:T(8,128)} %pad_maximum_fusion.p_ref), custom_call_target="tpu_custom_call" | custom-call | tf_op jit(solution)/shard_map/small_totals/pallas_call | solution.py:633
  604.4 1.2 slice.17
  605.6 1.3 slice_bitcast_fusion
  606.9 11.7 %copy.14 = f32[1024,4096]{1,0:T(8,128)} copy(f32[1024,4096]{1,0:T(8,128)} %get-tuple-element.40) | data formatting | bytes 33554432
  (23 shorter events, 0.1 us)
Async XLA Ops:
  0.6 6.8 %copy-start = (bf16[256,4096]{1,0:T(8,128)(2,1)S(1)}, bf16[256,4096]{1,0:T(8,128)(2,1)}, u32[]{:S(2)}) copy-start(bf16[256,4096]{1,0:T(8,128)(2,1)} %param.7) | copy-start | bytes 6291460
  0.6 6.8 %copy-start.3 = (f32[4096]{0:T(1024)S(1)}, f32[4096]{0:T(1024)}, u32[]{:S(2)}) copy-start(f32[4096]{0:T(1024)} %param.8) | copy-start | bytes 49156
  0.7 5.1 copy-start.13
  0.7 5.1 copy-start.14
  0.7 5.1 copy-start.12
  0.7 6.8 %copy-start.7 = (f32[4096]{0:T(1024)S(1)}, f32[4096]{0:T(1024)}, u32[]{:S(2)}) copy-start(f32[4096]{0:T(1024)} %param.9) | copy-start | bytes 49156
  2.9 4.6 copy-start.5
  5.2 0.6 copy-start.10
  5.7 1.7 copy-start.8
  211.2 367.8 %copy-start.4 = (f32[4096]{0:T(1024)S(1)}, f32[4096]{0:T(1024)}, u32[]{:S(2)}) copy-start(f32[4096]{0:T(1024)} %param.8) | copy-start | bytes 49156
  211.2 367.8 %copy-start.6 = (f32[256]{0:T(256)S(1)}, f32[256]{0:T(256)}, u32[]{:S(2)}) copy-start(f32[256]{0:T(256)} %copy-done.5) | copy-start | bytes 3076
  211.2 367.8 %copy-start.9 = (f32[256]{0:T(256)S(1)}, f32[256]{0:T(256)}, u32[]{:S(2)}) copy-start(f32[256]{0:T(256)} %copy-done.8) | copy-start | bytes 3076
  576.5 7.3 %copy-start.11 = (f32[256]{0:T(256)S(1)}, f32[256]{0:T(256)}, u32[]{:S(2)}) copy-start(f32[256]{0:T(256)} %copy-done.10) | copy-start | bytes 3076
  576.5 7.3 %copy-start.1 = (bf16[256,4096]{1,0:T(8,128)(2,1)S(1)}, bf16[256,4096]{1,0:T(8,128)(2,1)}, u32[]{:S(2)}) copy-start(bf16[256,4096]{1,0:T(8,128)(2,1)} %param.7) | copy-start | bytes 6291460
  576.5 7.3 %copy-start.2 = (f32[256,4096]{1,0:T(8,128)S(1)}, f32[256,4096]{1,0:T(8,128)}, u32[]{:S(2)}) copy-start(f32[256,4096]{1,0:T(8,128)} %get-tuple-element.22) | copy-start | bytes 12582916
